TPU v7x, 128 devices: a whole 4x4x4 slice. The times are simulated.
128 devices in a mesh: seq: 16 (over x, y), head: 8 (over z, core).
Axes of the slice: x: 4, y: 4, z: 4, core: 2. Of those that a mesh axis runs over, the one named last changes fastest.
Arguments:
- queries: bfloat16 [4096, 12288], P('seq', 'head'), may hold values from -256 to 256
- own_latent: bfloat16 [4096, 576], P('seq'), may hold values from -16 to 16
- cache: bfloat16 [512, 128, 576], P('seq', 'head'), may hold values from -6 to 6
- block_list: int32 [16, 32], replicated, may hold values from 0 to 511, as said below
- offsets: int32 [16, 32], P('seq'), may hold values from -4096 to 4096
- tile_mask: int32 [16, 2, 32], P('seq'), may hold values 0 or 1
- w_uk: bfloat16 [64, 128, 512], P('head'), may hold values from -0.5 to 0.5
- w_uv: bfloat16 [64, 512, 128], P('head'), may hold values from -0.25 to 0.25
- w_o: bfloat16 [8192, 7168], P('head'), may hold values from -0.0625 to 0.0625
Outputs:
- layer_out: bfloat16 [4096, 7168], P('seq', 'head')
Inputs may be any that keep to these rules, and one draw needn't show every extreme that they name: `block_list`: entry (r, j) names a pooled span whose owner is index entry // 32 of seq. In each row no owner is named more than 4 times, and at least one owner is named exactly 4 times.
All inputs are finite; a program needn't handle non-finite values. No bound on the sum of `tile_mask` on one device may be relied on, other than what follows from the above.
Results may differ from a plain program's by a relative error of at most 0.015.
Values may be sent and summed in bfloat16 or wider, within the bound.
No kernel may reach another device: no remote copies, remote signals or barrier semaphores. Data moves between devices by JAX's collectives and lax.ppermute only.
A program may use at most 128 MiB of HBM per device.

v0:
```python
import jax
import jax.numpy as jnp
from jax import lax
from jax.sharding import PartitionSpec as P

MOST = 4
THETA = 50000.0


def rerotate(blocks, shift, latent_width):
    rotary_width = blocks.shape[-1] - latent_width
    halfway = rotary_width // 2
    inverse = THETA ** (-jnp.arange(halfway, dtype=jnp.float32) * 2.0 / rotary_width)
    angles = shift.astype(jnp.float32)[:, None] * inverse[None, :]
    cosine_table = jnp.cos(angles)[:, None, :]
    sine_table = jnp.sin(angles)[:, None, :]
    rotary = blocks[..., latent_width:].astype(jnp.float32)
    first_half = rotary[..., :halfway]
    second_half = rotary[..., halfway:]
    turned = jnp.concatenate(
        [
            first_half * cosine_table - second_half * sine_table,
            second_half * cosine_table + first_half * sine_table,
        ],
        axis=-1,
    )
    return jnp.concatenate([blocks[..., :latent_width], turned.astype(jnp.bfloat16)], axis=-1)


def allowed_keys(tiles, query_rows, block_rows):
    listed_mask = jnp.repeat(jnp.repeat(tiles > 0, block_rows, axis=0), block_rows, axis=1)
    causal = jnp.tril(jnp.ones((query_rows, query_rows), jnp.bool_))
    return jnp.concatenate([causal, listed_mask], axis=1)


def attend(grouped, context, allowed, key_maps, value_maps):
    nope_width = key_maps.shape[1]
    latent_width = key_maps.shape[2]
    factor = grouped.shape[-1] ** (-0.5)
    value_latent = context[:, :latent_width]

    def one_head(inputs):
        head_query, key_map, value_map = inputs
        query_latent = jnp.dot(
            head_query[:, :nope_width], key_map, preferred_element_type=jnp.float32
        ).astype(jnp.bfloat16)
        query_full = jnp.concatenate([query_latent, head_query[:, nope_width:]], axis=1)
        scores = (
            lax.dot_general(
                query_full, context, (((1,), (1,)), ((), ())), preferred_element_type=jnp.float32
            )
            * factor
        )
        scores = jnp.where(allowed, scores, -1e30)
        highest = jnp.max(scores, axis=1, keepdims=True)
        weights = jnp.exp(scores - highest)
        denominator = jnp.sum(weights, axis=1, keepdims=True)
        shares = (weights / denominator).astype(jnp.bfloat16)
        mixed_latent = jnp.dot(shares, value_latent, preferred_element_type=jnp.float32).astype(
            jnp.bfloat16
        )
        return jnp.dot(mixed_latent, value_map, preferred_element_type=jnp.float32).astype(
            jnp.bfloat16
        )

    per_head = lax.map(one_head, (jnp.transpose(grouped, (1, 0, 2)), key_maps, value_maps))
    return jnp.transpose(per_head, (1, 0, 2)).reshape(grouped.shape[0], -1)


def per_device(queries, own_latent, cache, block_list, offsets, tile_mask, w_uk, w_uv, w_o):
    seq_count = lax.axis_size("seq")
    seq_index = lax.axis_index("seq")
    spans_held = cache.shape[0]
    latent_full = cache.shape[2]
    listed_count = block_list.shape[1]
    owners = block_list // spans_held
    within = block_list % spans_held
    earlier = jnp.tril(jnp.ones((listed_count, listed_count), jnp.bool_), -1)
    same_owner = owners[:, :, None] == owners[:, None, :]
    ranking = jnp.sum(same_owner & earlier[None], axis=2)
    slot_ids = jnp.arange(MOST, dtype=jnp.int32)
    matches = (owners == seq_index)[:, :, None] & (ranking[:, :, None] == slot_ids[None, None, :])
    send_index = jnp.sum(jnp.where(matches, within[:, :, None], 0), axis=1)
    my_owners = lax.dynamic_index_in_dim(owners, seq_index, 0, keepdims=False)
    my_ranking = lax.dynamic_index_in_dim(ranking, seq_index, 0, keepdims=False)
    flat_slot = my_owners * MOST + my_ranking
    arrived = lax.all_to_all(cache[send_index], "seq", split_axis=0, concat_axis=0, tiled=True)
    picked = arrived.reshape(seq_count * MOST, cache.shape[1], latent_full)[flat_slot]
    blocks = lax.all_gather(picked, "head", axis=1, tiled=True)
    latent_width = w_uk.shape[2]
    block_rows = blocks.shape[1]
    turned = rerotate(blocks, offsets[0], latent_width).reshape(
        listed_count * block_rows, latent_full
    )
    context = jnp.concatenate([own_latent, turned], axis=0)
    query_rows = own_latent.shape[0]
    allowed = allowed_keys(tile_mask[0], query_rows, block_rows)
    head_width = w_uk.shape[1] + latent_full - latent_width
    grouped = queries.reshape(query_rows, -1, head_width)
    head_out = attend(grouped, context, allowed, w_uk, w_uv)
    partial_value = jnp.dot(head_out, w_o, preferred_element_type=jnp.float32)
    result = lax.psum_scatter(
        partial_value.astype(jnp.bfloat16), "head", scatter_dimension=1, tiled=True
    )
    return result


def solution(mesh):
    placed = (
        P("seq", "head"),
        P("seq", None),
        P("seq", "head", None),
        P(),
        P("seq", None),
        P("seq", None, None),
        P("head", None, None),
        P("head", None, None),
        P("head", None),
    )
    return jax.shard_map(
        per_device, mesh=mesh, in_specs=placed, out_specs=P("seq", "head"), check_vma=False
    )
```

profile of v0, /device:TPU:0, one launch (start us, length us, event | category | flops | bytes accessed | tf_op | source)
XLA Modules:
  0.0 265.0 jit_solution(6012045879321765092)
XLA Ops:
  6.6 0.8 add_select_fusion
  7.3 0.7 broadcast_compare_fusion
  8.1 0.5 convert_reduce_fusion
  9.0 1.8 gather_fusion
  10.7 7.3 %all-to-all-start = ((bf16[16,4,16,576]{3,2,1,0:T(8,128)(2,1)}), bf16[16,4,16,576]{3,2,1,0:T(8,128)(2,1)S(1)}, u32[]{:S(2)}, u32[]{:S(2)}) async-start(bf16[16,4,16,576]{3,2,1,0:T(8,128)(2,1)} %bitcast.7), calls=%async_computation | async-start | bytes 2621440 | tf_op jit(solution)/shard_map/all_to_all | solution.py:87
  18.1 20.7 %all-to-all-done = bf16[16,4,16,576]{3,2,1,0:T(8,128)(2,1)S(1)} async-done(((bf16[16,4,16,576]{3,2,1,0:T(8,128)(2,1)}), bf16[16,4,16,576]{3,2,1,0:T(8,128)(2,1)S(1)}, u32[]{:S(2)}, u32[]{:S(2)}) %all-to-all-start) | async-done | bytes 1179680 | tf_op jit(solution)/shard_map/all_to_all | solution.py:87
  38.8 1.5 gather_fusion.1
  40.4 0.2 copy.24
  40.6 2.1 broadcast_in_dim.33
  42.7 0.7 copy.34
  43.5 0.3 copy.22
  44.0 1.4 pad_add_fusion
  45.4 30.7 %all-gather.3.cloned.1.call-done = bf16[32,128,576]{2,1,0:T(8,128)(2,1)} async-done(((bf16[32,16,576]{2,1,0:T(8,128)(2,1)}), bf16[32,128,576]{2,1,0:T(8,128)(2,1)}) %all-gather.3.cloned.1.call-update) | async-done | bytes 4718608 | tf_op jit(solution)/shard_map/all_gather | solution.py:89
  76.0 1.5 slice_convert_fusion
  77.5 0.9 subtract_convert_fusion
  78.4 2.2 slice-done
  80.6 1.1 pad_maximum_fusion.1
  81.7 2.9 %pad_maximum_fusion = bf16[4352,576]{1,0:T(8,128)(2,1)} fusion(bf16[256,576]{1,0:T(8,128)(2,1)S(1)} %copy.24, bf16[4096,576]{1,0:T(8,128)(2,1)S(1)} %bitcast.53), kind=kLoop, calls=%fused_computation.28 | loop fusion | flops 10027008 | bytes 10027008 | tf_op jit(solution)/shard_map/concatenate | solution.py:95
  84.7 2.5 fusion.18
  87.1 115.0 %while.10 = (s32[]{:T(128)}, bf16[8,256,128]{1,2,0:T(8,128)(2,1)S(1)}, bf16[8,256,192]{1,2,0:T(8,128)(2,1)S(1)}, bf16[8,128,512]{2,1,0:T(8,128)(2,1)}, bf16[4352...) while((s32[]{:T(128)}, ...), condition=%wide.region_5.6_spmd, body=%wide.region_2.5_spmd.sunk | while | flops 2501213696 | bytes 43456640 | solution.py:66
  87.3 1.1 convolution_convert_fusion.3
  88.4 4.9 %fusion.41 = (f32[256]{0:T(256)S(1)}, f32[256,4352]{1,0:T(8,128)S(1)}) fusion(pred[256,4352]{1,0:T(32,128)(4,1)} %get-tuple-element.172, bf16[4352,576]{1,0:T(8,128)(2,1)} %get-tuple-element.171, bf16[256,64]{1,0:T(8,128)(2,1)S(1)} %slice.54, bf16[256,512]{1,0:T(8,128)(2,1)S(1)} %convolution_convert_fusion.3), kind=kOutput, calls=%fused_computation.63.clone.1 | convolution fusion | flops 1287388928 | bytes 10880000 | tf_op jit(solution)/shard_map/while/body/eval_jaxpr/dot_general | solution.py:49
  93.3 2.1 copy-done.2
  95.5 0.7 fusion.42
  96.2 5.1 %fusion.43 = bf16[1,256,128]{2,1,0:T(8,128)(2,1)S(1)} fusion(bf16[4352,512]{1,0:T(8,128)(2,1)} %get-tuple-element.173, f32[256,4352]{1,0:T(8,128)} %copy-done.2, f32[256]{0:T(256)S(1)} %fusion.42, f32[256]{0:T(256)S(1)} %get-tuple-element.148, bf16[8,512,128]{2,1,0:T(8,128)(2,1)} %get-tuple-element.174, s32[]{:T(128)} %get-tuple-element.158), kind=kOutput, calls=%fused_computation.12.clone.1 | convolution fusion | flops 1177911296 | bytes 9112064 | tf_op jit(solution)/shard_map/while/body/eval_jaxpr/dot_general | solution.py:62
  101.6 1.1 convolution_convert_fusion.3
  102.8 4.9 %fusion.41 = (f32[256]{0:T(256)S(1)}, f32[256,4352]{1,0:T(8,128)S(1)}) fusion(pred[256,4352]{1,0:T(32,128)(4,1)} %get-tuple-element.172, bf16[4352,576]{1,0:T(8,128)(2,1)} %get-tuple-element.171, bf16[256,64]{1,0:T(8,128)(2,1)S(1)} %slice.54, bf16[256,512]{1,0:T(8,128)(2,1)S(1)} %convolution_convert_fusion.3), kind=kOutput, calls=%fused_computation.63.clone.1 | convolution fusion | flops 1287388928 | bytes 10880000 | tf_op jit(solution)/shard_map/while/body/eval_jaxpr/dot_general | solution.py:49
  107.7 2.1 copy-done.2
  109.9 0.7 fusion.42
  110.6 5.1 %fusion.43 = bf16[1,256,128]{2,1,0:T(8,128)(2,1)S(1)} fusion(bf16[4352,512]{1,0:T(8,128)(2,1)} %get-tuple-element.173, f32[256,4352]{1,0:T(8,128)} %copy-done.2, f32[256]{0:T(256)S(1)} %fusion.42, f32[256]{0:T(256)S(1)} %get-tuple-element.148, bf16[8,512,128]{2,1,0:T(8,128)(2,1)} %get-tuple-element.174, s32[]{:T(128)} %get-tuple-element.158), kind=kOutput, calls=%fused_computation.12.clone.1 | convolution fusion | flops 1177911296 | bytes 9112064 | tf_op jit(solution)/shard_map/while/body/eval_jaxpr/dot_general | solution.py:62
  116.0 1.1 convolution_convert_fusion.3
  117.2 4.9 %fusion.41 = (f32[256]{0:T(256)S(1)}, f32[256,4352]{1,0:T(8,128)S(1)}) fusion(pred[256,4352]{1,0:T(32,128)(4,1)} %get-tuple-element.172, bf16[4352,576]{1,0:T(8,128)(2,1)} %get-tuple-element.171, bf16[256,64]{1,0:T(8,128)(2,1)S(1)} %slice.54, bf16[256,512]{1,0:T(8,128)(2,1)S(1)} %convolution_convert_fusion.3), kind=kOutput, calls=%fused_computation.63.clone.1 | convolution fusion | flops 1287388928 | bytes 10880000 | tf_op jit(solution)/shard_map/while/body/eval_jaxpr/dot_general | solution.py:49
  122.1 2.1 copy-done.2
  124.2 0.7 fusion.42
  125.0 5.1 %fusion.43 = bf16[1,256,128]{2,1,0:T(8,128)(2,1)S(1)} fusion(bf16[4352,512]{1,0:T(8,128)(2,1)} %get-tuple-element.173, f32[256,4352]{1,0:T(8,128)} %copy-done.2, f32[256]{0:T(256)S(1)} %fusion.42, f32[256]{0:T(256)S(1)} %get-tuple-element.148, bf16[8,512,128]{2,1,0:T(8,128)(2,1)} %get-tuple-element.174, s32[]{:T(128)} %get-tuple-element.158), kind=kOutput, calls=%fused_computation.12.clone.1 | convolution fusion | flops 1177911296 | bytes 9112064 | tf_op jit(solution)/shard_map/while/body/eval_jaxpr/dot_general | solution.py:62
  130.4 1.1 convolution_convert_fusion.3
  131.5 4.9 %fusion.41 = (f32[256]{0:T(256)S(1)}, f32[256,4352]{1,0:T(8,128)S(1)}) fusion(pred[256,4352]{1,0:T(32,128)(4,1)} %get-tuple-element.172, bf16[4352,576]{1,0:T(8,128)(2,1)} %get-tuple-element.171, bf16[256,64]{1,0:T(8,128)(2,1)S(1)} %slice.54, bf16[256,512]{1,0:T(8,128)(2,1)S(1)} %convolution_convert_fusion.3), kind=kOutput, calls=%fused_computation.63.clone.1 | convolution fusion | flops 1287388928 | bytes 10880000 | tf_op jit(solution)/shard_map/while/body/eval_jaxpr/dot_general | solution.py:49
  136.5 2.1 copy-done.2
  138.6 0.7 fusion.42
  139.4 5.1 %fusion.43 = bf16[1,256,128]{2,1,0:T(8,128)(2,1)S(1)} fusion(bf16[4352,512]{1,0:T(8,128)(2,1)} %get-tuple-element.173, f32[256,4352]{1,0:T(8,128)} %copy-done.2, f32[256]{0:T(256)S(1)} %fusion.42, f32[256]{0:T(256)S(1)} %get-tuple-element.148, bf16[8,512,128]{2,1,0:T(8,128)(2,1)} %get-tuple-element.174, s32[]{:T(128)} %get-tuple-element.158), kind=kOutput, calls=%fused_computation.12.clone.1 | convolution fusion | flops 1177911296 | bytes 9112064 | tf_op jit(solution)/shard_map/while/body/eval_jaxpr/dot_general | solution.py:62
  144.8 1.1 convolution_convert_fusion.3
  145.9 4.9 %fusion.41 = (f32[256]{0:T(256)S(1)}, f32[256,4352]{1,0:T(8,128)S(1)}) fusion(pred[256,4352]{1,0:T(32,128)(4,1)} %get-tuple-element.172, bf16[4352,576]{1,0:T(8,128)(2,1)} %get-tuple-element.171, bf16[256,64]{1,0:T(8,128)(2,1)S(1)} %slice.54, bf16[256,512]{1,0:T(8,128)(2,1)S(1)} %convolution_convert_fusion.3), kind=kOutput, calls=%fused_computation.63.clone.1 | convolution fusion | flops 1287388928 | bytes 10880000 | tf_op jit(solution)/shard_map/while/body/eval_jaxpr/dot_general | solution.py:49
  150.9 2.1 copy-done.2
  153.0 0.7 fusion.42
  153.7 5.1 %fusion.43 = bf16[1,256,128]{2,1,0:T(8,128)(2,1)S(1)} fusion(bf16[4352,512]{1,0:T(8,128)(2,1)} %get-tuple-element.173, f32[256,4352]{1,0:T(8,128)} %copy-done.2, f32[256]{0:T(256)S(1)} %fusion.42, f32[256]{0:T(256)S(1)} %get-tuple-element.148, bf16[8,512,128]{2,1,0:T(8,128)(2,1)} %get-tuple-element.174, s32[]{:T(128)} %get-tuple-element.158), kind=kOutput, calls=%fused_computation.12.clone.1 | convolution fusion | flops 1177911296 | bytes 9112064 | tf_op jit(solution)/shard_map/while/body/eval_jaxpr/dot_general | solution.py:62
  159.2 1.1 convolution_convert_fusion.3
  160.3 4.9 %fusion.41 = (f32[256]{0:T(256)S(1)}, f32[256,4352]{1,0:T(8,128)S(1)}) fusion(pred[256,4352]{1,0:T(32,128)(4,1)} %get-tuple-element.172, bf16[4352,576]{1,0:T(8,128)(2,1)} %get-tuple-element.171, bf16[256,64]{1,0:T(8,128)(2,1)S(1)} %slice.54, bf16[256,512]{1,0:T(8,128)(2,1)S(1)} %convolution_convert_fusion.3), kind=kOutput, calls=%fused_computation.63.clone.1 | convolution fusion | flops 1287388928 | bytes 10880000 | tf_op jit(solution)/shard_map/while/body/eval_jaxpr/dot_general | solution.py:49
  165.3 2.1 copy-done.2
  167.4 0.7 fusion.42
  168.1 5.1 %fusion.43 = bf16[1,256,128]{2,1,0:T(8,128)(2,1)S(1)} fusion(bf16[4352,512]{1,0:T(8,128)(2,1)} %get-tuple-element.173, f32[256,4352]{1,0:T(8,128)} %copy-done.2, f32[256]{0:T(256)S(1)} %fusion.42, f32[256]{0:T(256)S(1)} %get-tuple-element.148, bf16[8,512,128]{2,1,0:T(8,128)(2,1)} %get-tuple-element.174, s32[]{:T(128)} %get-tuple-element.158), kind=kOutput, calls=%fused_computation.12.clone.1 | convolution fusion | flops 1177911296 | bytes 9112064 | tf_op jit(solution)/shard_map/while/body/eval_jaxpr/dot_general | solution.py:62
  173.6 1.1 convolution_convert_fusion.3
  174.7 4.9 %fusion.41 = (f32[256]{0:T(256)S(1)}, f32[256,4352]{1,0:T(8,128)S(1)}) fusion(pred[256,4352]{1,0:T(32,128)(4,1)} %get-tuple-element.172, bf16[4352,576]{1,0:T(8,128)(2,1)} %get-tuple-element.171, bf16[256,64]{1,0:T(8,128)(2,1)S(1)} %slice.54, bf16[256,512]{1,0:T(8,128)(2,1)S(1)} %convolution_convert_fusion.3), kind=kOutput, calls=%fused_computation.63.clone.1 | convolution fusion | flops 1287388928 | bytes 10880000 | tf_op jit(solution)/shard_map/while/body/eval_jaxpr/dot_general | solution.py:49
  179.6 2.1 copy-done.2
  181.8 0.7 fusion.42
  182.5 5.1 %fusion.43 = bf16[1,256,128]{2,1,0:T(8,128)(2,1)S(1)} fusion(bf16[4352,512]{1,0:T(8,128)(2,1)} %get-tuple-element.173, f32[256,4352]{1,0:T(8,128)} %copy-done.2, f32[256]{0:T(256)S(1)} %fusion.42, f32[256]{0:T(256)S(1)} %get-tuple-element.148, bf16[8,512,128]{2,1,0:T(8,128)(2,1)} %get-tuple-element.174, s32[]{:T(128)} %get-tuple-element.158), kind=kOutput, calls=%fused_computation.12.clone.1 | convolution fusion | flops 1177911296 | bytes 9112064 | tf_op jit(solution)/shard_map/while/body/eval_jaxpr/dot_general | solution.py:62
  187.9 1.1 convolution_convert_fusion.3
  189.1 4.9 %fusion.41 = (f32[256]{0:T(256)S(1)}, f32[256,4352]{1,0:T(8,128)S(1)}) fusion(pred[256,4352]{1,0:T(32,128)(4,1)} %get-tuple-element.172, bf16[4352,576]{1,0:T(8,128)(2,1)} %get-tuple-element.171, bf16[256,64]{1,0:T(8,128)(2,1)S(1)} %slice.54, bf16[256,512]{1,0:T(8,128)(2,1)S(1)} %convolution_convert_fusion.3), kind=kOutput, calls=%fused_computation.63.clone.1 | convolution fusion | flops 1287388928 | bytes 10880000 | tf_op jit(solution)/shard_map/while/body/eval_jaxpr/dot_general | solution.py:49
  194.0 2.1 copy-done.2
  196.1 0.7 fusion.42
  196.9 5.1 %fusion.43 = bf16[1,256,128]{2,1,0:T(8,128)(2,1)S(1)} fusion(bf16[4352,512]{1,0:T(8,128)(2,1)} %get-tuple-element.173, f32[256,4352]{1,0:T(8,128)} %copy-done.2, f32[256]{0:T(256)S(1)} %fusion.42, f32[256]{0:T(256)S(1)} %get-tuple-element.148, bf16[8,512,128]{2,1,0:T(8,128)(2,1)} %get-tuple-element.174, s32[]{:T(128)} %get-tuple-element.158), kind=kOutput, calls=%fused_computation.12.clone.1 | convolution fusion | flops 1177911296 | bytes 9112064 | tf_op jit(solution)/shard_map/while/body/eval_jaxpr/dot_general | solution.py:62
  202.2 10.9 %convolution_convert_fusion.1 = bf16[256,7168]{1,0:T(8,128)(2,1)} fusion(bf16[256,1024]{0,1:T(8,128)(2,1)S(1)} %bitcast.62, bf16[1024,7168]{1,0:T(8,128)(2,1)} %param.19), kind=kOutput, calls=%fused_computation.26 | convolution fusion | flops 3759931392 | bytes 18874368 | tf_op jit(solution)/shard_map/dot_general | solution.py:101
  213.1 5.9 %copy.27 = bf16[256,7168]{0,1:T(8,128)(2,1)} copy(bf16[256,7168]{1,0:T(8,128)(2,1)} %convolution_convert_fusion.1) | data formatting | bytes 7340032
  219.0 37.2 %reduce-scatter.4.cloned.1.call-done = bf16[896,256]{1,0:T(8,128)(2,1)} async-done(((bf16[7168,256]{1,0:T(8,128)(2,1)}), bf16[896,256]{1,0:T(8,128)(2,1)}) %reduce-scatter.4.cloned.1.call-update) | async-done | bytes 458768
  256.2 2.0 copy.28
  (83 shorter events, 2.7 us)
Async XLA Ops:
  6.5 2.4 copy-start
  6.5 33.9 %copy-start.5 = (bf16[256,576]{0,1:T(8,128)(2,1)S(1)}, bf16[256,576]{0,1:T(8,128)(2,1)}, u32[]{:S(2)}) copy-start(bf16[256,576]{0,1:T(8,128)(2,1)} %param.12) | copy-start | bytes 884740
  6.5 34.1 %copy-start.6 = (s32[1,2,32]{2,1,0:T(2,128)S(1)}, s32[1,2,32]{2,1,0:T(2,128)}, u32[]{:S(2)}) copy-start(s32[1,2,32]{2,1,0:T(2,128)} %param.16) | copy-start | bytes 772
  10.7 32.7 %copy-start.3 = (bf16[256,1536]{1,0:T(8,128)(2,1)S(1)}, bf16[256,1536]{1,0:T(8,128)(2,1)}, u32[]{:S(2)}) copy-start(bf16[256,1536]{1,0:T(8,128)(2,1)} %param.11) | copy-start | bytes 2359300
  10.7 33.1 %copy-start.7 = (s32[1,32]{1,0:T(1,128)S(1)}, s32[1,32]{1,0:T(1,128)}, u32[]{:S(2)}) copy-start(s32[1,32]{1,0:T(1,128)} %param.15) | copy-start | bytes 388
  10.7 28.1 %all-to-all-start = ((bf16[16,4,16,576]{3,2,1,0:T(8,128)(2,1)}), bf16[16,4,16,576]{3,2,1,0:T(8,128)(2,1)S(1)}, u32[]{:S(2)}, u32[]{:S(2)}) async-start(bf16[16,4,16,576]{3,2,1,0:T(8,128)(2,1)} %bitcast.7), calls=%async_computation | async-start | bytes 2621440 | tf_op jit(solution)/shard_map/all_to_all | solution.py:87
  18.0 58.0 %all-gather.3.cloned.1.call-start = ((), (), s32[]{:S(2)}) async-start(), calls=%async_computation.2 | async-start | bytes 5898240 | tf_op jit(solution)/shard_map/all_gather | solution.py:89
  40.3 215.9 %reduce-scatter.4.cloned.1.call-start = ((), (), s32[]{:S(2)}) async-start(), calls=%async_computation.3 | async-start | bytes 4128768
  78.4 2.2 slice-start
  84.7 2.5 copy-start.4
  93.3 2.1 copy-start.2
  107.7 2.1 copy-start.2
  122.1 2.1 copy-start.2
  136.5 2.1 copy-start.2
  150.9 2.1 copy-start.2
  165.2 2.1 copy-start.2
  179.6 2.1 copy-start.2
  194.0 2.1 copy-start.2
  202.2 56.0 %copy-start.1 = (bf16[32,16,576]{2,1,0:T(8,128)(2,1)S(1)}, bf16[32,16,576]{2,1,0:T(8,128)(2,1)}, u32[]{:S(2)}) copy-start(bf16[32,16,576]{2,1,0:T(8,128)(2,1)} %param.13) | copy-start | bytes 1769476
Sparse Core Ops, SparseCore 0:
  40.5 35.5 all-gather.2
  219.1 37.0 reduce-scatter.3
where the time goes:
time: 266 us; the launch traced here: 265 us
  matrix products  100 us (38%)
  waiting for transfers between devices  88.6 us (33%)
  local copies, waits for them, and re-layouts  35.9 us (13%)
  other arithmetic  18.6 us (7%)
  between operations  13.6 us (5%)
  starting transfers between devices  7.36 us (3%)
    dot_general x8, matrix products, one_head(): jnp.dot(mixed_latent, value_map, preferred_element_type=jnp.float32)  41.1 us
    dot_general x8, matrix products, one_head(): lax.dot_general(query_full, context, (((1,), (1,)), ((), ())), preferred_...  39.5 us
    unnamed x3, waiting for transfers between devices  37.2 us
    all_gather x1, waiting for transfers between devices, per_device(): blocks = lax.all_gather(picked, 'head', axis=1, tiled=True)  30.7 us
    all_to_all x1, waiting for transfers between devices, per_device(): lax.all_to_all(cache[send_index], 'seq', split_axis=0, concat_axis=0, til...  20.7 us
    while x16, local copies, waits for them, and re-layouts  17.1 us
    dot_general x1, matrix products, per_device(): partial_value = jnp.dot(head_out, w_o, preferred_element_type=jnp.float32)  10.9 us
    unnamed x19, local copies, waits for them, and re-layouts  9.16 us
  transfers between devices with their start and end apart: 3, of which 3 were waited for; matrix products, arithmetic and copies ran while one was open for 2% of the time, Pallas kernels for 0%

commit v1 on v0

--- a/solution.py
+++ b/solution.py
@@ -86,7 +86,7 @@
     flat_slot = my_owners * MOST + my_ranking
     arrived = lax.all_to_all(cache[send_index], "seq", split_axis=0, concat_axis=0, tiled=True)
     picked = arrived.reshape(seq_count * MOST, cache.shape[1], latent_full)[flat_slot]
-    blocks = lax.all_gather(picked, "head", axis=1, tiled=True)
+    blocks = jnp.concatenate(lax.all_gather(picked, "head"), axis=1)
     latent_width = w_uk.shape[2]
     block_rows = blocks.shape[1]
     turned = rerotate(blocks, offsets[0], latent_width).reshape(

time: 266 us -> 266 us (level)
    reshape x0 -> x1, local copies, waits for them, and re-layouts: none -> 3.29 us  [per_device(): blocks = jnp.concatenate(lax.all_gather(picked, 'head'), axis=1)]
where the time goes in v1:
time: 266 us; the launch traced here: 265 us
  matrix products  100 us (38%)
  waiting for transfers between devices  88.6 us (33%)
  local copies, waits for them, and re-layouts  37.3 us (14%)
  other arithmetic  17.4 us (7%)
  between operations  13.6 us (5%)
  starting transfers between devices  7.36 us (3%)
    dot_general x8, matrix products, one_head(): jnp.dot(mixed_latent, value_map, preferred_element_type=jnp.float32)  41.1 us
    dot_general x8, matrix products, one_head(): lax.dot_general(query_full, context, (((1,), (1,)), ((), ())), preferred_...  39.5 us
    unnamed x3, waiting for transfers between devices  37.2 us
    all_gather x1, waiting for transfers between devices, per_device(): blocks = jnp.concatenate(lax.all_gather(picked, 'head'), axis=1)  30.7 us
    all_to_all x1, waiting for transfers between devices, per_device(): lax.all_to_all(cache[send_index], 'seq', split_axis=0, concat_axis=0, til...  20.7 us
    while x16, local copies, waits for them, and re-layouts  17 us
    dot_general x1, matrix products, per_device(): partial_value = jnp.dot(head_out, w_o, preferred_element_type=jnp.float32)  11 us
    unnamed x19, local copies, waits for them, and re-layouts  9.15 us
  transfers between devices with their start and end apart: 3, of which 3 were waited for; matrix products, arithmetic and copies ran while one was open for 2% of the time, Pallas kernels for 0%

profile of v1, /device:TPU:0, one launch (start us, length us, event | category | flops | bytes accessed | tf_op | source)
XLA Modules:
  0.0 265.5 jit_solution(8601492594841205187)
XLA Ops:
  6.6 0.8 add_select_fusion
  7.3 0.7 broadcast_compare_fusion
  8.1 0.5 convert_reduce_fusion
  9.0 1.8 gather_fusion
  10.7 7.3 %all-to-all-start = ((bf16[16,4,16,576]{3,2,1,0:T(8,128)(2,1)}), bf16[16,4,16,576]{3,2,1,0:T(8,128)(2,1)S(1)}, u32[]{:S(2)}, u32[]{:S(2)}) async-start(bf16[16,4,16,576]{3,2,1,0:T(8,128)(2,1)} %bitcast.7), calls=%async_computation | async-start | bytes 2621440 | tf_op jit(solution)/shard_map/all_to_all | solution.py:87
  18.1 20.7 %all-to-all-done = bf16[16,4,16,576]{3,2,1,0:T(8,128)(2,1)S(1)} async-done(((bf16[16,4,16,576]{3,2,1,0:T(8,128)(2,1)}), bf16[16,4,16,576]{3,2,1,0:T(8,128)(2,1)S(1)}, u32[]{:S(2)}, u32[]{:S(2)}) %all-to-all-start) | async-done | bytes 1179680 | tf_op jit(solution)/shard_map/all_to_all | solution.py:87
  38.8 1.5 gather_fusion.1
  40.7 2.1 broadcast_in_dim.33
  42.7 0.7 copy.42
  43.5 0.3 copy.29
  44.0 1.4 pad_add_fusion
  45.4 30.7 %all-gather.3.cloned.1.call-done = bf16[256,16,576]{2,1,0:T(8,128)(2,1)} async-done(((bf16[32,16,576]{2,1,0:T(8,128)(2,1)}), bf16[256,16,576]{2,1,0:T(8,128)(2,1)}) %all-gather.3.cloned.1.call-update) | async-done | bytes 4718608 | tf_op jit(solution)/shard_map/all_gather | solution.py:89
  76.1 3.3 %copy.31 = bf16[32,8,16,576]{3,2,1,0:T(8,128)(2,1)S(1)} copy(bf16[32,8,16,576]{3,2,0,1:T(8,128)(2,1)} %bitcast.64) | data formatting | bytes 9437184 | tf_op jit(solution)/shard_map/reshape | solution.py:89
  79.4 0.3 slice_convert_fusion
  79.6 0.4 slice.32
  80.0 0.9 subtract_convert_fusion
  81.0 1.1 pad_maximum_fusion.1
  82.1 3.0 %pad_maximum_fusion = bf16[4352,576]{1,0:T(8,128)(2,1)} fusion(bf16[256,576]{1,0:T(8,128)(2,1)S(1)} %copy.32, bf16[4096,576]{1,0:T(8,128)(2,1)S(1)} %bitcast.57), kind=kLoop, calls=%fused_computation.28 | loop fusion | flops 10027008 | bytes 10027008 | tf_op jit(solution)/shard_map/concatenate | solution.py:95
  85.0 2.5 fusion.18
  87.5 115.0 %while.10 = (s32[]{:T(128)}, bf16[8,256,128]{1,2,0:T(8,128)(2,1)S(1)}, bf16[8,256,192]{1,2,0:T(8,128)(2,1)S(1)}, bf16[8,128,512]{2,1,0:T(8,128)(2,1)}, bf16[4352...) while((s32[]{:T(128)}, ...), condition=%wide.region_5.6_spmd, body=%wide.region_2.5_spmd.sunk | while | flops 2501213696 | bytes 43456640 | solution.py:66
  87.6 1.1 convolution_convert_fusion.3
  88.8 4.9 %fusion.41 = (f32[256]{0:T(256)S(1)}, f32[256,4352]{1,0:T(8,128)S(1)}) fusion(pred[256,4352]{1,0:T(32,128)(4,1)} %get-tuple-element.180, bf16[4352,576]{1,0:T(8,128)(2,1)} %get-tuple-element.179, bf16[256,64]{1,0:T(8,128)(2,1)S(1)} %slice.54, bf16[256,512]{1,0:T(8,128)(2,1)S(1)} %convolution_convert_fusion.3), kind=kOutput, calls=%fused_computation.63.clone.1 | convolution fusion | flops 1287388928 | bytes 10880000 | tf_op jit(solution)/shard_map/while/body/eval_jaxpr/dot_general | solution.py:49
  93.7 2.1 copy-done.2
  95.9 0.7 fusion.42
  96.6 5.1 %fusion.43 = bf16[1,256,128]{2,1,0:T(8,128)(2,1)S(1)} fusion(bf16[4352,512]{1,0:T(8,128)(2,1)} %get-tuple-element.181, f32[256,4352]{1,0:T(8,128)} %copy-done.2, f32[256]{0:T(256)S(1)} %fusion.42, f32[256]{0:T(256)S(1)} %get-tuple-element.156, bf16[8,512,128]{2,1,0:T(8,128)(2,1)} %get-tuple-element.182, s32[]{:T(128)} %get-tuple-element.166), kind=kOutput, calls=%fused_computation.12.clone.1 | convolution fusion | flops 1177911296 | bytes 9112064 | tf_op jit(solution)/shard_map/while/body/eval_jaxpr/dot_general | solution.py:62
  102.0 1.1 convolution_convert_fusion.3
  103.2 4.9 %fusion.41 = (f32[256]{0:T(256)S(1)}, f32[256,4352]{1,0:T(8,128)S(1)}) fusion(pred[256,4352]{1,0:T(32,128)(4,1)} %get-tuple-element.180, bf16[4352,576]{1,0:T(8,128)(2,1)} %get-tuple-element.179, bf16[256,64]{1,0:T(8,128)(2,1)S(1)} %slice.54, bf16[256,512]{1,0:T(8,128)(2,1)S(1)} %convolution_convert_fusion.3), kind=kOutput, calls=%fused_computation.63.clone.1 | convolution fusion | flops 1287388928 | bytes 10880000 | tf_op jit(solution)/shard_map/while/body/eval_jaxpr/dot_general | solution.py:49
  108.1 2.1 copy-done.2
  110.2 0.7 fusion.42
  111.0 5.1 %fusion.43 = bf16[1,256,128]{2,1,0:T(8,128)(2,1)S(1)} fusion(bf16[4352,512]{1,0:T(8,128)(2,1)} %get-tuple-element.181, f32[256,4352]{1,0:T(8,128)} %copy-done.2, f32[256]{0:T(256)S(1)} %fusion.42, f32[256]{0:T(256)S(1)} %get-tuple-element.156, bf16[8,512,128]{2,1,0:T(8,128)(2,1)} %get-tuple-element.182, s32[]{:T(128)} %get-tuple-element.166), kind=kOutput, calls=%fused_computation.12.clone.1 | convolution fusion | flops 1177911296 | bytes 9112064 | tf_op jit(solution)/shard_map/while/body/eval_jaxpr/dot_general | solution.py:62
  116.4 1.1 convolution_convert_fusion.3
  117.5 4.9 %fusion.41 = (f32[256]{0:T(256)S(1)}, f32[256,4352]{1,0:T(8,128)S(1)}) fusion(pred[256,4352]{1,0:T(32,128)(4,1)} %get-tuple-element.180, bf16[4352,576]{1,0:T(8,128)(2,1)} %get-tuple-element.179, bf16[256,64]{1,0:T(8,128)(2,1)S(1)} %slice.54, bf16[256,512]{1,0:T(8,128)(2,1)S(1)} %convolution_convert_fusion.3), kind=kOutput, calls=%fused_computation.63.clone.1 | convolution fusion | flops 1287388928 | bytes 10880000 | tf_op jit(solution)/shard_map/while/body/eval_jaxpr/dot_general | solution.py:49
  122.5 2.1 copy-done.2
  124.6 0.7 fusion.42
  125.3 5.1 %fusion.43 = bf16[1,256,128]{2,1,0:T(8,128)(2,1)S(1)} fusion(bf16[4352,512]{1,0:T(8,128)(2,1)} %get-tuple-element.181, f32[256,4352]{1,0:T(8,128)} %copy-done.2, f32[256]{0:T(256)S(1)} %fusion.42, f32[256]{0:T(256)S(1)} %get-tuple-element.156, bf16[8,512,128]{2,1,0:T(8,128)(2,1)} %get-tuple-element.182, s32[]{:T(128)} %get-tuple-element.166), kind=kOutput, calls=%fused_computation.12.clone.1 | convolution fusion | flops 1177911296 | bytes 9112064 | tf_op jit(solution)/shard_map/while/body/eval_jaxpr/dot_general | solution.py:62
  130.8 1.1 convolution_convert_fusion.3
  131.9 4.9 %fusion.41 = (f32[256]{0:T(256)S(1)}, f32[256,4352]{1,0:T(8,128)S(1)}) fusion(pred[256,4352]{1,0:T(32,128)(4,1)} %get-tuple-element.180, bf16[4352,576]{1,0:T(8,128)(2,1)} %get-tuple-element.179, bf16[256,64]{1,0:T(8,128)(2,1)S(1)} %slice.54, bf16[256,512]{1,0:T(8,128)(2,1)S(1)} %convolution_convert_fusion.3), kind=kOutput, calls=%fused_computation.63.clone.1 | convolution fusion | flops 1287388928 | bytes 10880000 | tf_op jit(solution)/shard_map/while/body/eval_jaxpr/dot_general | solution.py:49
  136.8 2.1 copy-done.2
  139.0 0.7 fusion.42
  139.7 5.1 %fusion.43 = bf16[1,256,128]{2,1,0:T(8,128)(2,1)S(1)} fusion(bf16[4352,512]{1,0:T(8,128)(2,1)} %get-tuple-element.181, f32[256,4352]{1,0:T(8,128)} %copy-done.2, f32[256]{0:T(256)S(1)} %fusion.42, f32[256]{0:T(256)S(1)} %get-tuple-element.156, bf16[8,512,128]{2,1,0:T(8,128)(2,1)} %get-tuple-element.182, s32[]{:T(128)} %get-tuple-element.166), kind=kOutput, calls=%fused_computation.12.clone.1 | convolution fusion | flops 1177911296 | bytes 9112064 | tf_op jit(solution)/shard_map/while/body/eval_jaxpr/dot_general | solution.py:62
  145.1 1.1 convolution_convert_fusion.3
  146.3 4.9 %fusion.41 = (f32[256]{0:T(256)S(1)}, f32[256,4352]{1,0:T(8,128)S(1)}) fusion(pred[256,4352]{1,0:T(32,128)(4,1)} %get-tuple-element.180, bf16[4352,576]{1,0:T(8,128)(2,1)} %get-tuple-element.179, bf16[256,64]{1,0:T(8,128)(2,1)S(1)} %slice.54, bf16[256,512]{1,0:T(8,128)(2,1)S(1)} %convolution_convert_fusion.3), kind=kOutput, calls=%fused_computation.63.clone.1 | convolution fusion | flops 1287388928 | bytes 10880000 | tf_op jit(solution)/shard_map/while/body/eval_jaxpr/dot_general | solution.py:49
  151.2 2.1 copy-done.2
  153.3 0.7 fusion.42
  154.1 5.1 %fusion.43 = bf16[1,256,128]{2,1,0:T(8,128)(2,1)S(1)} fusion(bf16[4352,512]{1,0:T(8,128)(2,1)} %get-tuple-element.181, f32[256,4352]{1,0:T(8,128)} %copy-done.2, f32[256]{0:T(256)S(1)} %fusion.42, f32[256]{0:T(256)S(1)} %get-tuple-element.156, bf16[8,512,128]{2,1,0:T(8,128)(2,1)} %get-tuple-element.182, s32[]{:T(128)} %get-tuple-element.166), kind=kOutput, calls=%fused_computation.12.clone.1 | convolution fusion | flops 1177911296 | bytes 9112064 | tf_op jit(solution)/shard_map/while/body/eval_jaxpr/dot_general | solution.py:62
  159.5 1.1 convolution_convert_fusion.3
  160.6 4.9 %fusion.41 = (f32[256]{0:T(256)S(1)}, f32[256,4352]{1,0:T(8,128)S(1)}) fusion(pred[256,4352]{1,0:T(32,128)(4,1)} %get-tuple-element.180, bf16[4352,576]{1,0:T(8,128)(2,1)} %get-tuple-element.179, bf16[256,64]{1,0:T(8,128)(2,1)S(1)} %slice.54, bf16[256,512]{1,0:T(8,128)(2,1)S(1)} %convolution_convert_fusion.3), kind=kOutput, calls=%fused_computation.63.clone.1 | convolution fusion | flops 1287388928 | bytes 10880000 | tf_op jit(solution)/shard_map/while/body/eval_jaxpr/dot_general | solution.py:49
  165.6 2.1 copy-done.2
  167.7 0.7 fusion.42
  168.5 5.1 %fusion.43 = bf16[1,256,128]{2,1,0:T(8,128)(2,1)S(1)} fusion(bf16[4352,512]{1,0:T(8,128)(2,1)} %get-tuple-element.181, f32[256,4352]{1,0:T(8,128)} %copy-done.2, f32[256]{0:T(256)S(1)} %fusion.42, f32[256]{0:T(256)S(1)} %get-tuple-element.156, bf16[8,512,128]{2,1,0:T(8,128)(2,1)} %get-tuple-element.182, s32[]{:T(128)} %get-tuple-element.166), kind=kOutput, calls=%fused_computation.12.clone.1 | convolution fusion | flops 1177911296 | bytes 9112064 | tf_op jit(solution)/shard_map/while/body/eval_jaxpr/dot_general | solution.py:62
  173.9 1.1 convolution_convert_fusion.3
  175.0 4.9 %fusion.41 = (f32[256]{0:T(256)S(1)}, f32[256,4352]{1,0:T(8,128)S(1)}) fusion(pred[256,4352]{1,0:T(32,128)(4,1)} %get-tuple-element.180, bf16[4352,576]{1,0:T(8,128)(2,1)} %get-tuple-element.179, bf16[256,64]{1,0:T(8,128)(2,1)S(1)} %slice.54, bf16[256,512]{1,0:T(8,128)(2,1)S(1)} %convolution_convert_fusion.3), kind=kOutput, calls=%fused_computation.63.clone.1 | convolution fusion | flops 1287388928 | bytes 10880000 | tf_op jit(solution)/shard_map/while/body/eval_jaxpr/dot_general | solution.py:49
  180.0 2.1 copy-done.2
  182.1 0.7 fusion.42
  182.8 5.1 %fusion.43 = bf16[1,256,128]{2,1,0:T(8,128)(2,1)S(1)} fusion(bf16[4352,512]{1,0:T(8,128)(2,1)} %get-tuple-element.181, f32[256,4352]{1,0:T(8,128)} %copy-done.2, f32[256]{0:T(256)S(1)} %fusion.42, f32[256]{0:T(256)S(1)} %get-tuple-element.156, bf16[8,512,128]{2,1,0:T(8,128)(2,1)} %get-tuple-element.182, s32[]{:T(128)} %get-tuple-element.166), kind=kOutput, calls=%fused_computation.12.clone.1 | convolution fusion | flops 1177911296 | bytes 9112064 | tf_op jit(solution)/shard_map/while/body/eval_jaxpr/dot_general | solution.py:62
  188.3 1.1 convolution_convert_fusion.3
  189.4 4.9 %fusion.41 = (f32[256]{0:T(256)S(1)}, f32[256,4352]{1,0:T(8,128)S(1)}) fusion(pred[256,4352]{1,0:T(32,128)(4,1)} %get-tuple-element.180, bf16[4352,576]{1,0:T(8,128)(2,1)} %get-tuple-element.179, bf16[256,64]{1,0:T(8,128)(2,1)S(1)} %slice.54, bf16[256,512]{1,0:T(8,128)(2,1)S(1)} %convolution_convert_fusion.3), kind=kOutput, calls=%fused_computation.63.clone.1 | convolution fusion | flops 1287388928 | bytes 10880000 | tf_op jit(solution)/shard_map/while/body/eval_jaxpr/dot_general | solution.py:49
  194.3 2.1 copy-done.2
  196.5 0.7 fusion.42
  197.2 5.1 %fusion.43 = bf16[1,256,128]{2,1,0:T(8,128)(2,1)S(1)} fusion(bf16[4352,512]{1,0:T(8,128)(2,1)} %get-tuple-element.181, f32[256,4352]{1,0:T(8,128)} %copy-done.2, f32[256]{0:T(256)S(1)} %fusion.42, f32[256]{0:T(256)S(1)} %get-tuple-element.156, bf16[8,512,128]{2,1,0:T(8,128)(2,1)} %get-tuple-element.182, s32[]{:T(128)} %get-tuple-element.166), kind=kOutput, calls=%fused_computation.12.clone.1 | convolution fusion | flops 1177911296 | bytes 9112064 | tf_op jit(solution)/shard_map/while/body/eval_jaxpr/dot_general | solution.py:62
  202.5 11.0 %convolution_convert_fusion.1 = bf16[256,7168]{1,0:T(8,128)(2,1)} fusion(bf16[256,1024]{0,1:T(8,128)(2,1)S(1)} %bitcast.69, bf16[1024,7168]{1,0:T(8,128)(2,1)} %param.19), kind=kOutput, calls=%fused_computation.26 | convolution fusion | flops 3759931392 | bytes 18874368 | tf_op jit(solution)/shard_map/dot_general | solution.py:101
  213.5 5.9 %copy.35 = bf16[256,7168]{0,1:T(8,128)(2,1)} copy(bf16[256,7168]{1,0:T(8,128)(2,1)} %convolution_convert_fusion.1) | data formatting | bytes 7340032
  219.4 37.2 %reduce-scatter.4.cloned.1.call-done = bf16[896,256]{1,0:T(8,128)(2,1)} async-done(((bf16[7168,256]{1,0:T(8,128)(2,1)}), bf16[896,256]{1,0:T(8,128)(2,1)}) %reduce-scatter.4.cloned.1.call-update) | async-done | bytes 458768
  256.6 2.0 copy.36
  (83 shorter events, 2.9 us)
Async XLA Ops:
  6.5 2.4 copy-start
  6.5 33.9 %copy-start.5 = (bf16[256,576]{0,1:T(8,128)(2,1)S(1)}, bf16[256,576]{0,1:T(8,128)(2,1)}, u32[]{:S(2)}) copy-start(bf16[256,576]{0,1:T(8,128)(2,1)} %param.12) | copy-start | bytes 884740
  6.5 34.1 %copy-start.6 = (s32[1,2,32]{2,1,0:T(2,128)S(1)}, s32[1,2,32]{2,1,0:T(2,128)}, u32[]{:S(2)}) copy-start(s32[1,2,32]{2,1,0:T(2,128)} %param.16) | copy-start | bytes 772
  10.7 32.8 %copy-start.3 = (bf16[256,1536]{1,0:T(8,128)(2,1)S(1)}, bf16[256,1536]{1,0:T(8,128)(2,1)}, u32[]{:S(2)}) copy-start(bf16[256,1536]{1,0:T(8,128)(2,1)} %param.11) | copy-start | bytes 2359300
  10.7 33.1 %copy-start.7 = (s32[1,32]{1,0:T(1,128)S(1)}, s32[1,32]{1,0:T(1,128)}, u32[]{:S(2)}) copy-start(s32[1,32]{1,0:T(1,128)} %param.15) | copy-start | bytes 388
  10.7 28.1 %all-to-all-start = ((bf16[16,4,16,576]{3,2,1,0:T(8,128)(2,1)}), bf16[16,4,16,576]{3,2,1,0:T(8,128)(2,1)S(1)}, u32[]{:S(2)}, u32[]{:S(2)}) async-start(bf16[16,4,16,576]{3,2,1,0:T(8,128)(2,1)} %bitcast.7), calls=%async_computation | async-start | bytes 2621440 | tf_op jit(solution)/shard_map/all_to_all | solution.py:87
  18.0 58.0 %all-gather.3.cloned.1.call-start = ((), (), s32[]{:S(2)}) async-start(), calls=%async_computation.2 | async-start | bytes 5898240 | tf_op jit(solution)/shard_map/all_gather | solution.py:89
  40.4 216.3 %reduce-scatter.4.cloned.1.call-start = ((), (), s32[]{:S(2)}) async-start(), calls=%async_computation.3 | async-start | bytes 4128768
  85.0 2.5 copy-start.4
  93.7 2.1 copy-start.2
  108.1 2.1 copy-start.2
  122.5 2.1 copy-start.2
  136.8 2.1 copy-start.2
  151.2 2.1 copy-start.2
  165.6 2.1 copy-start.2
  180.0 2.1 copy-start.2
  194.3 2.1 copy-start.2
  202.5 56.1 %copy-start.1 = (bf16[32,16,576]{2,1,0:T(8,128)(2,1)S(1)}, bf16[32,16,576]{2,1,0:T(8,128)(2,1)}, u32[]{:S(2)}) copy-start(bf16[32,16,576]{2,1,0:T(8,128)(2,1)} %param.13) | copy-start | bytes 1769476
Sparse Core Ops, SparseCore 0:
  40.5 35.5 all-gather.2
  219.6 37.0 reduce-scatter.3
